TPU v7x, 32 devices: a whole 2x2x4 slice. The times are simulated.
32 devices in a mesh: dp: 16 (over z, x, core), tensor: 2 (over y).
Axes of the slice: x: 2, y: 2, z: 4, core: 2. Of those that a mesh axis runs over, the one named last changes fastest.
Arguments:
- inputs: bfloat16 [64, 320, 1024], P(('dp', 'tensor')), may hold values from -6 to 6
- lengths: int32 [64], P('dp'), may hold values from 224 to 320, as said below
- cotangent: bfloat16 [64, 320, 1024], P(('dp', 'tensor')), may hold values from -6 to 6
- first_gain: bfloat16 [1024], P(('dp', 'tensor')), may hold values from 0.25 to 1.75
- first_shift: bfloat16 [1024], P(('dp', 'tensor')), may hold values from -2 to 2
- qkv_weight: bfloat16 [3, 1024, 1024], P(None, 'dp', 'tensor'), may hold values from -0.1875 to 0.1875
- query_bias: bfloat16 [1024], P(('dp', 'tensor')), may hold values from -3 to 3
- value_bias: bfloat16 [1024], P(('dp', 'tensor')), may hold values from -3 to 3
- out_weight: bfloat16 [1024, 1024], P('tensor', 'dp'), may hold values from -1.5 to 1.5
- out_bias: bfloat16 [1024], P(('dp', 'tensor')), may hold values from -3 to 3
- second_gain: bfloat16 [1024], P(('dp', 'tensor')), may hold values from 0.25 to 1.75
- second_shift: bfloat16 [1024], P(('dp', 'tensor')), may hold values from -2 to 2
- up_weight: bfloat16 [1024, 4096], P('dp', 'tensor'), may hold values from -0.1875 to 0.1875
- up_bias: bfloat16 [4096], P(('dp', 'tensor')), may hold values from -3 to 3
- down_weight: bfloat16 [4096, 1024], P('tensor', 'dp'), may hold values from -0.09375 to 0.09375
- down_bias: bfloat16 [1024], P(('dp', 'tensor')), may hold values from -3 to 3
Outputs:
- output: bfloat16 [64, 320, 1024], P(('dp', 'tensor'))
- input_grad: float32 [64, 320, 1024], P(('dp', 'tensor'))
- first_gain_grad: float32 [1024], P(('dp', 'tensor'))
- first_shift_grad: float32 [1024], P(('dp', 'tensor'))
- qkv_weight_grad: float32 [3, 1024, 1024], P(None, 'dp', 'tensor')
- query_bias_grad: float32 [1024], P(('dp', 'tensor'))
- value_bias_grad: float32 [1024], P(('dp', 'tensor'))
- out_weight_grad: float32 [1024, 1024], P('tensor', 'dp')
- out_bias_grad: float32 [1024], P(('dp', 'tensor'))
- second_gain_grad: float32 [1024], P(('dp', 'tensor'))
- second_shift_grad: float32 [1024], P(('dp', 'tensor'))
- up_weight_grad: float32 [1024, 4096], P('dp', 'tensor')
- up_bias_grad: float32 [4096], P(('dp', 'tensor'))
- down_weight_grad: float32 [4096, 1024], P('tensor', 'dp')
- down_bias_grad: float32 [1024], P(('dp', 'tensor'))
Inputs may be any that keep to these rules, and one draw needn't show every extreme that they name: lengths holds the number of valid slots of each image, counted from its first slot; slots from there on are padding.
All inputs are finite; a program needn't handle non-finite values.
Results may differ from a plain program's by a relative error of at most 0.017.
Values may be sent and summed in bfloat16 or wider, within the bound.
A program may use at most 192 MiB of HBM per device.

v0:
```python
import jax
import jax.numpy as jnp
from jax import lax
from jax.sharding import PartitionSpec as P

HEAD_DIM = 64
EPSILON = 1e-06
BOTH = ("dp", "tensor")
bf16 = jnp.bfloat16
f32 = jnp.float32


def exact_gelu(values):
    return jax.nn.gelu(values, approximate=False)


def norm_stats(values):
    average = jnp.mean(values, axis=-1, keepdims=True)
    centered = values - average
    variance = jnp.mean(centered * centered, axis=-1, keepdims=True)
    scale = lax.rsqrt(variance + EPSILON)
    return (centered * scale, scale)


def norm_back(grad, unit, scale, gain):
    z = grad * gain
    mean_z = jnp.mean(z, axis=-1, keepdims=True)
    mean_zx = jnp.mean(z * unit, axis=-1, keepdims=True)
    return scale * (z - mean_z - unit * mean_zx)


def gather_matrix(shard):
    wide = lax.all_gather(shard, "tensor", axis=1, tiled=True)
    return lax.all_gather(wide, "dp", axis=0, tiled=True)


def scatter_matrix(grad):
    rows, columns = grad.shape
    halves = jnp.stack(jnp.split(grad, lax.axis_size("tensor"), axis=1))
    halves = halves.reshape(-1, columns // lax.axis_size("tensor"))
    return lax.psum_scatter(halves, ("tensor", "dp"), scatter_dimension=0, tiled=True)


def mm(a, b, dims):
    return lax.dot_general(a, b, (dims, ((), ())), preferred_element_type=f32)


NN = ((1,), (0,))
NT = ((1,), (1,))
TN = ((0,), (0,))


def shards(
    inputs,
    lengths,
    cotangent,
    first_gain,
    first_shift,
    qkv_weight,
    query_bias,
    value_bias,
    out_weight,
    out_bias,
    second_gain,
    second_shift,
    up_weight,
    up_bias,
    down_weight,
    down_bias,
):
    image_count, slot_count, width = inputs.shape
    tensor_rank = lax.axis_index("tensor")
    heads = width // HEAD_DIM
    tokens = image_count * slot_count
    score_scale = HEAD_DIM ** (-0.5)
    device_count = lax.axis_size("dp") * lax.axis_size("tensor")
    vectors = (
        first_gain,
        first_shift,
        query_bias,
        value_bias,
        out_bias,
        second_gain,
        second_shift,
        down_bias,
        up_bias,
    )
    sizes = [v.shape[0] for v in vectors]
    packed = lax.all_gather(jnp.concatenate(vectors), BOTH, axis=0)
    full = []
    start = 0
    for size in sizes:
        full.append(packed[:, start : start + size].reshape(-1).astype(f32))
        start += size
    gain_one, shift_one, qbias, vbias, obias, gain_two, shift_two, dbias, ubias = full
    query_w = gather_matrix(qkv_weight[0])
    key_w = gather_matrix(qkv_weight[1])
    value_w = gather_matrix(qkv_weight[2])
    out_t = gather_matrix(out_weight.T)
    up_w = gather_matrix(up_weight)
    down_t = gather_matrix(down_weight.T)
    positions = jnp.arange(slot_count, dtype=jnp.int32)
    own_lengths = lax.dynamic_slice_in_dim(lengths, tensor_rank * image_count, image_count)
    valid = positions[None, :] < own_lengths[:, None]
    valid_rows = valid.astype(f32).reshape(tokens, 1)
    masked = inputs.reshape(tokens, width).astype(f32) * valid_rows
    unit_one, scale_one = norm_stats(masked)
    first = (unit_one * gain_one + shift_one).astype(bf16)

    def split(rows):
        return rows.reshape(image_count, slot_count, heads, HEAD_DIM)

    query = split((mm(first, query_w, NN) + qbias).astype(bf16))
    key = split(mm(first, key_w, NN).astype(bf16))
    value = split((mm(first, value_w, NN) + vbias).astype(bf16))
    scores = jnp.einsum("bqhc,bkhc->bhqk", query, key, preferred_element_type=f32) * score_scale
    scores = jnp.where(valid[:, None, None, :], scores, -1000000000.0)
    highest = jnp.max(scores, axis=-1, keepdims=True)
    shifted = jnp.exp(scores - highest)
    probs = shifted / jnp.sum(shifted, axis=-1, keepdims=True)
    weights_low = probs.astype(bf16)
    mixed = jnp.einsum("bhqk,bkhc->bqhc", weights_low, value, preferred_element_type=f32)
    mixed = mixed.astype(bf16).reshape(tokens, width)
    middle = masked + mm(mixed, out_t, NT) + obias
    unit_two, scale_two = norm_stats(middle)
    second = (unit_two * gain_two + shift_two).astype(bf16)
    hidden = mm(second, up_w, NN) + ubias
    active = exact_gelu(hidden).astype(bf16)
    output = (middle + mm(active, down_t, NT) + dbias).astype(bf16)
    grad_low = cotangent.reshape(tokens, width)
    grad_out = grad_low.astype(f32)
    down_grad = scatter_matrix(mm(grad_low, active, TN).astype(bf16))
    grad_active = mm(grad_low, down_t, NN)
    grad_hidden32 = jax.vjp(exact_gelu, hidden)[1](grad_active)[0]
    grad_hidden = grad_hidden32.astype(bf16)
    up_grad = scatter_matrix(mm(second, grad_hidden, TN).astype(bf16))
    grad_second = mm(grad_hidden, up_w, NT)
    grad_middle = grad_out + norm_back(grad_second, unit_two, scale_two, gain_two)
    grad_attn = grad_middle.astype(bf16)
    out_grad = scatter_matrix(mm(grad_attn, mixed, TN).astype(bf16))
    grad_mixed = split(mm(grad_attn, out_t, NN).astype(bf16))
    grad_weights = jnp.einsum("bqhc,bkhc->bhqk", grad_mixed, value, preferred_element_type=f32)
    value_grad = jnp.einsum("bhqk,bqhc->bkhc", weights_low, grad_mixed, preferred_element_type=f32)
    value_grad = value_grad.astype(bf16).reshape(tokens, width)
    inner = jnp.sum(probs * grad_weights, axis=-1, keepdims=True)
    grad_scores = (probs * (grad_weights - inner)).astype(bf16)
    query_grad = (
        jnp.einsum("bhqk,bkhc->bqhc", grad_scores, key, preferred_element_type=f32) * score_scale
    )
    key_grad = (
        jnp.einsum("bhqk,bqhc->bkhc", grad_scores, query, preferred_element_type=f32) * score_scale
    )
    query_grad = query_grad.astype(bf16).reshape(tokens, width)
    key_grad = key_grad.astype(bf16).reshape(tokens, width)
    qkv_grad = jnp.stack(
        [
            scatter_matrix(mm(first, query_grad, TN).astype(bf16)),
            scatter_matrix(mm(first, key_grad, TN).astype(bf16)),
            scatter_matrix(mm(first, value_grad, TN).astype(bf16)),
        ]
    )
    grad_first = mm(query_grad, query_w, NT) + mm(key_grad, key_w, NT) + mm(value_grad, value_w, NT)
    grad_in = norm_back(grad_first, unit_one, scale_one, gain_one)
    input_grad = (grad_middle + grad_in) * valid_rows

    def total(values):
        return jnp.sum(values.astype(f32), axis=0)

    vector_grads = (
        total(grad_first * unit_one),
        total(grad_first),
        total(query_grad),
        total(value_grad),
        total(grad_attn),
        total(grad_second * unit_two),
        total(grad_second),
        total(grad_low),
        total(grad_hidden),
    )
    stacked = jnp.concatenate([v.reshape(device_count, -1) for v in vector_grads], axis=1)
    own = lax.psum_scatter(stacked, BOTH, scatter_dimension=0, tiled=True)[0]
    shares = []
    start = 0
    for size in sizes:
        shares.append(own[start : start + size])
        start += size
    return (
        output.reshape(inputs.shape),
        input_grad.reshape(inputs.shape),
        shares[0],
        shares[1],
        qkv_grad.astype(f32),
        shares[2],
        shares[3],
        out_grad.T.astype(f32),
        shares[4],
        shares[5],
        shares[6],
        up_grad.astype(f32),
        shares[8],
        down_grad.T.astype(f32),
        shares[7],
    )


def solution(mesh):
    rows = P(BOTH, None, None)
    vector = P(BOTH)
    return jax.shard_map(
        shards,
        mesh=mesh,
        in_specs=(
            rows,
            P("dp"),
            rows,
            vector,
            vector,
            P(None, "dp", "tensor"),
            vector,
            vector,
            P("tensor", "dp"),
            vector,
            vector,
            vector,
            P("dp", "tensor"),
            vector,
            P("tensor", "dp"),
            vector,
        ),
        out_specs=(
            rows,
            rows,
            vector,
            vector,
            P(None, "dp", "tensor"),
            vector,
            vector,
            P("tensor", "dp"),
            vector,
            vector,
            vector,
            P("dp", "tensor"),
            vector,
            P("tensor", "dp"),
            vector,
        ),
        check_vma=False,
    )
```

profile of v0, /device:TPU:0, one launch (start us, length us, event | category | flops | bytes accessed | tf_op | source)
XLA Modules:
  0.0 1265.5 jit_solution(6776043386296748097)
XLA Ops:
  8.4 6.0 all-gather.5
  14.5 5.0 all-gather.1
  19.6 5.0 all-gather.3
  24.7 7.3 all_gather.50
  32.1 9.3 all_gather.52
  41.5 7.3 all_gather.54
  50.6 65.8 %all-gather.7 = bf16[32,1,384]{2,1,0:T(2,128)(2,1)S(1)} all-gather(bf16[1,1,384]{2,1,0:T(2,128)(2,1)S(1)} %reshape.425), channel_id=2, replica_groups=mesh['dp'=16,'tensor'=2] {'dp','tensor'}, dimensions={0}, use_global_device_ids=true | all-gather | bytes 25344 | tf_op jit(solution)/shard_map/all_gather | solution.py:89
  133.1 5.2 add_convert_fusion.5
  161.5 11.1 fusion.63
  172.6 7.6 fusion.45
  190.6 69.1 %all-gather.17.cloned.1.call-done = bf16[1024,4096]{1,0:T(8,128)(2,1)} async-done(((bf16[64,4096]{1,0:T(8,128)(2,1)}), bf16[1024,4096]{1,0:T(8,128)(2,1)}) %all-gather.17.cloned.1.call-update) | async-done | bytes 8388624 | tf_op jit(solution)/shard_map/all_gather | solution.py:34
  259.7 11.4 fusion.60
  271.1 63.5 %all-gather.19.cloned.1.call-done = bf16[1024,4096]{1,0:T(8,128)(2,1)} async-done(((bf16[64,4096]{1,0:T(8,128)(2,1)}), bf16[1024,4096]{1,0:T(8,128)(2,1)}) %all-gather.19.cloned.1.call-update) | async-done | bytes 8388624 | tf_op jit(solution)/shard_map/all_gather | solution.py:34
  334.7 35.0 %convert_reduce_fusion = (f32[4096]{0:T(1024)}, bf16[640,4096]{1,0:T(8,128)(2,1)S(1)}, f32[640,4096]{1,0:T(8,128)}) fusion(f32[640,4096]{1,0:T(8,128)} %fusion.60, f32[4096]{0:T(1024)S(1)} %fusion.54, bf16[640,1024]{1,0:T(8,128)(2,1)} %bitcast.173, bf16[1024,4096]{1,0:T(8,128)(2,1)} %all-gather.19.cloned.1.call-done), kind=kOutput, calls=%fused_computation.8 | convolution fusion | flops 5565313024 | bytes 35946496 | tf_op jit(solution)/shard_map/dot_general | solution.py:45
  369.7 6.1 multiply_reduce_fusion.1
  385.6 5.0 copy.72
  390.5 8.6 convert_reduce_fusion.1
  411.8 14.3 %multiply_reduce_fusion = (f32[2,16,320]{2,1,0:T(8,128)S(1)}, f32[2,16,320,320]{2,3,1,0:T(8,128)}) fusion(f32[2,16,320,320]{2,3,1,0:T(8,128)} %get-tuple-element.62, f32[2,16,320]{2,1,0:T(8,128)S(1)} %get-tuple-element.61, bf16[2,320,16,64]{1,3,2,0:T(8,128)(2,1)} %copy.72, bf16[2,320,16,64]{1,3,2,0:T(8,128)(2,1)} %copy.68), kind=kOutput, calls=%fused_computation.2 | convolution fusion | flops 429250560 | bytes 28917760 | tf_op jit(solution)/shard_map/bqhc,bkhc->bhqk/dot_general | solution.py:142
  426.1 11.2 multiply_convert_fusion
  453.0 5.4 convert_reduce_fusion.2
  477.3 9.7 convolution_convert_fusion
  489.4 6.2 pad_maximum_fusion
  495.7 8.2 multiply_convert_fusion.1
  504.0 7.3 convert_bitcast_fusion
  513.7 6.2 pad_maximum_fusion.1
  531.4 39.9 %all-reduce = f32[32,384]{1,0:T(8,128)S(1)} all-reduce(f32[32,384]{1,0:T(8,128)S(1)} %concatenate.7), channel_id=9, replica_groups=mesh['dp'=16,'tensor'=2] {'dp','tensor'}, use_global_device_ids=true, to_apply=%region_20.21.clone | all-reduce | flops 12288 | bytes 98304
  576.8 10.5 add_convert_fusion.2
  587.3 98.5 %reduce-scatter.9.cloned.1.call-done = bf16[64,512]{1,0:T(8,128)(2,1)} async-done(((bf16[2048,512]{1,0:T(8,128)(2,1)}), bf16[64,512]{1,0:T(8,128)(2,1)}) %reduce-scatter.9.cloned.1.call-update) | async-done | bytes 65552 | tf_op jit(solution)/shard_map/reduce_scatter | solution.py:41
  685.8 136.7 %reduce-scatter.7.cloned.1.call-done = bf16[64,512]{1,0:T(8,128)(2,1)} async-done(((bf16[2048,512]{1,0:T(8,128)(2,1)}), bf16[64,512]{1,0:T(8,128)(2,1)}) %reduce-scatter.7.cloned.1.call-update) | async-done | bytes 65552 | tf_op jit(solution)/shard_map/reduce_scatter | solution.py:41
  824.2 134.9 %reduce-scatter.13.cloned.1.call-done = bf16[64,512]{1,0:T(8,128)(2,1)} async-done(((bf16[2048,512]{1,0:T(8,128)(2,1)}), bf16[64,512]{1,0:T(8,128)(2,1)}) %reduce-scatter.13.cloned.1.call-update) | async-done | bytes 65552 | tf_op jit(solution)/shard_map/reduce_scatter | solution.py:41
  960.6 147.0 %reduce-scatter.15.cloned.1.call-done = bf16[64,2048]{1,0:T(8,128)(2,1)} async-done(((bf16[2048,2048]{1,0:T(8,128)(2,1)}), bf16[64,2048]{1,0:T(8,128)(2,1)}) %reduce-scatter.15.cloned.1.call-update) | async-done | bytes 262160 | tf_op jit(solution)/shard_map/reduce_scatter | solution.py:41
  1109.4 147.2 %reduce-scatter.17.cloned.1.call-done = bf16[64,2048]{1,0:T(8,128)(2,1)} async-done(((bf16[2048,2048]{1,0:T(8,128)(2,1)}), bf16[64,2048]{1,0:T(8,128)(2,1)}) %reduce-scatter.17.cloned.1.call-update) | async-done | bytes 262160 | tf_op jit(solution)/shard_map/reduce_scatter | solution.py:41
  (201 shorter events, 138.5 us)
Async XLA Ops:
  7.2 34.3 %copy-start.15 = (bf16[2048,64]{0,1:T(8,128)(2,1)S(1)}, bf16[2048,64]{0,1:T(8,128)(2,1)}, u32[]{:S(2)}) copy-start(bf16[2048,64]{0,1:T(8,128)(2,1)} %param.30) | copy-start | bytes 786436
  7.2 41.8 %copy-start.35 = (bf16[32]{0:T(256)(128)(2,1)S(1)}, bf16[32]{0:T(256)(128)(2,1)}, u32[]{:S(2)}) copy-start(bf16[32]{0:T(256)(128)(2,1)} %param.31) | copy-start | bytes 196
  7.2 41.8 %copy-start.36 = (bf16[128]{0:T(256)(128)(2,1)S(1)}, bf16[128]{0:T(256)(128)(2,1)}, u32[]{:S(2)}) copy-start(bf16[128]{0:T(256)(128)(2,1)} %param.29) | copy-start | bytes 772
  7.2 41.8 %copy-start.34 = (bf16[32]{0:T(256)(128)(2,1)S(1)}, bf16[32]{0:T(256)(128)(2,1)}, u32[]{:S(2)}) copy-start(bf16[32]{0:T(256)(128)(2,1)} %param.27) | copy-start | bytes 196
  7.2 41.8 %copy-start.33 = (bf16[32]{0:T(256)(128)(2,1)S(1)}, bf16[32]{0:T(256)(128)(2,1)}, u32[]{:S(2)}) copy-start(bf16[32]{0:T(256)(128)(2,1)} %param.26) | copy-start | bytes 196
  7.2 41.8 %copy-start.32 = (bf16[32]{0:T(256)(128)(2,1)S(1)}, bf16[32]{0:T(256)(128)(2,1)}, u32[]{:S(2)}) copy-start(bf16[32]{0:T(256)(128)(2,1)} %param.25) | copy-start | bytes 196
  7.2 41.8 %copy-start.31 = (bf16[32]{0:T(256)(128)(2,1)S(1)}, bf16[32]{0:T(256)(128)(2,1)}, u32[]{:S(2)}) copy-start(bf16[32]{0:T(256)(128)(2,1)} %param.23) | copy-start | bytes 196
  7.3 41.8 %copy-start.30 = (bf16[32]{0:T(256)(128)(2,1)S(1)}, bf16[32]{0:T(256)(128)(2,1)}, u32[]{:S(2)}) copy-start(bf16[32]{0:T(256)(128)(2,1)} %param.22) | copy-start | bytes 196
  7.3 41.8 %copy-start.29 = (bf16[32]{0:T(256)(128)(2,1)S(1)}, bf16[32]{0:T(256)(128)(2,1)}, u32[]{:S(2)}) copy-start(bf16[32]{0:T(256)(128)(2,1)} %param.20) | copy-start | bytes 196
  7.3 41.8 %copy-start.28 = (bf16[32]{0:T(256)(128)(2,1)S(1)}, bf16[32]{0:T(256)(128)(2,1)}, u32[]{:S(2)}) copy-start(bf16[32]{0:T(256)(128)(2,1)} %param.19) | copy-start | bytes 196
  7.3 41.9 %copy-start.41 = (s32[4]{0:T(128)S(1)}, s32[4]{0:T(128)}, u32[]{:S(2)}) copy-start(s32[4]{0:T(128)} %param.17) | copy-start | bytes 52
  7.3 42.1 %copy-start.1 = (bf16[2,320,1024]{2,1,0:T(8,128)(2,1)S(1)}, bf16[2,320,1024]{2,1,0:T(8,128)(2,1)}, u32[]{:S(2)}) copy-start(bf16[2,320,1024]{2,1,0:T(8,128)(2,1)} %param.16) | copy-start | bytes 3932164
  7.3 112.7 %all-gather.25.cloned.1.call-start = ((), (), s32[]{:S(2)}) async-start(), calls=%async_computation.17 | async-start | bytes 2228224 | tf_op jit(solution)/shard_map/all_gather | solution.py:34
  14.4 118.7 %all-gather.21.cloned.1.call-start = ((), (), s32[]{:S(2)}) async-start(), calls=%async_computation.15 | async-start | bytes 2228224 | tf_op jit(solution)/shard_map/all_gather | solution.py:34
  19.5 128.0 %all-gather.23.cloned.1.call-start = ((), (), s32[]{:S(2)}) async-start(), calls=%async_computation.16 | async-start | bytes 2228224 | tf_op jit(solution)/shard_map/all_gather | solution.py:34
  24.7 160.0 %all-gather.15.cloned.1.call-start = ((), (), s32[]{:S(2)}) async-start(), calls=%async_computation.6 | async-start | bytes 2228224 | tf_op jit(solution)/shard_map/all_gather | solution.py:34
  32.1 227.6 %all-gather.17.cloned.1.call-start = ((), (), s32[]{:S(2)}) async-start(), calls=%async_computation.7 | async-start | bytes 8912896 | tf_op jit(solution)/shard_map/all_gather | solution.py:34
  41.5 293.2 %all-gather.19.cloned.1.call-start = ((), (), s32[]{:S(2)}) async-start(), calls=%async_computation.8 | async-start | bytes 8912896 | tf_op jit(solution)/shard_map/all_gather | solution.py:34
  48.9 538.4 %reduce-scatter.11.cloned.1.call-start = ((), (), s32[]{:S(2)}) async-start(), calls=%async_computation.11 | async-start | bytes 2162688 | tf_op jit(solution)/shard_map/reduce_scatter | solution.py:41
  49.4 135.3 %copy-start.19 = (f32[640]{0:T(1024)}, f32[640]{0:T(1024)S(1)}, u32[]{:S(2)}) copy-start(f32[640]{0:T(1024)S(1)} %reshape.408) | copy-start | bytes 7684
  49.9 70.0 %copy-start.21 = (f32[640]{0:T(1024)}, f32[640]{0:T(1024)S(1)}, u32[]{:S(2)}) copy-start(f32[640]{0:T(1024)S(1)} %div.35) | copy-start | bytes 7684
  50.6 69.4 %copy-start.23 = (f32[640]{0:T(1024)}, f32[640]{0:T(1024)S(1)}, u32[]{:S(2)}) copy-start(f32[640]{0:T(1024)S(1)} %rsqrt.21) | copy-start | bytes 7684
  117.3 142.4 %copy-start.26 = (f32[1024]{0:T(1024)}, f32[1024]{0:T(1024)S(1)}, u32[]{:S(2)}) copy-start(f32[1024]{0:T(1024)S(1)} %reshape.415) | copy-start | bytes 12292
  133.1 28.4 %copy-start.7 = (bf16[2,320,16,64]{1,3,2,0:T(8,128)(2,1)}, bf16[2,320,16,64]{1,3,2,0:T(8,128)(2,1)S(1)}, u32[]{:S(2)}) copy-start(bf16[2,320,16,64]{1,3,2,0:T(8,128)(2,1)S(1)} %copy.67) | copy-start | bytes 3932164
  334.6 35.0 %copy-start.4 = (f32[640,1024]{1,0:T(8,128)S(1)}, f32[640,1024]{1,0:T(8,128)}, u32[]{:S(2)}) copy-start(f32[640,1024]{1,0:T(8,128)} %copy-done.3) | copy-start | bytes 7864324
  334.7 35.0 %copy-start.37 = (bf16[1024,4096]{1,0:T(8,128)(2,1)S(1)}, bf16[1024,4096]{1,0:T(8,128)(2,1)}, u32[]{:S(2)}) copy-start(bf16[1024,4096]{1,0:T(8,128)(2,1)} %all-gather.17.cloned.1.call-done) | copy-start | bytes 25165828
  411.7 274.1 %reduce-scatter.9.cloned.1.call-start = ((), (), s32[]{:S(2)}) async-start(), calls=%async_computation.10 | async-start | bytes 2162688 | tf_op jit(solution)/shard_map/reduce_scatter | solution.py:41
  426.1 11.2 copy-start.8
  453.0 369.6 %reduce-scatter.7.cloned.1.call-start = ((), (), s32[]{:S(2)}) async-start(), calls=%async_computation.9 | async-start | bytes 2162688 | tf_op jit(solution)/shard_map/reduce_scatter | solution.py:41
  471.4 487.7 %reduce-scatter.13.cloned.1.call-start = ((), (), s32[]{:S(2)}) async-start(), calls=%async_computation.12 | async-start | bytes 2162688 | tf_op jit(solution)/shard_map/reduce_scatter | solution.py:41
  477.2 630.4 %reduce-scatter.15.cloned.1.call-start = ((), (), s32[]{:S(2)}) async-start(), calls=%async_computation.13 | async-start | bytes 8650752 | tf_op jit(solution)/shard_map/reduce_scatter | solution.py:41
  495.7 761.0 %reduce-scatter.17.cloned.1.call-start = ((), (), s32[]{:S(2)}) async-start(), calls=%async_computation.14 | async-start | bytes 8650752 | tf_op jit(solution)/shard_map/reduce_scatter | solution.py:41
  (23 other events, 74.7 us)
Sparse Core Ops, SparseCore 0:
  14.5 43.2 all-gather.24
  60.0 40.1 all-gather.20
  102.4 40.0 all-gather.22
  144.5 40.1 all-gather.14
  186.7 73.0 all-gather.16
  261.7 72.8 all-gather.18
  411.9 137.0 reduce-scatter.10
  551.3 134.4 reduce-scatter.8
  688.1 134.4 reduce-scatter.6
  824.6 134.4 reduce-scatter.12
  961.4 146.1 reduce-scatter.14
  1109.8 146.8 reduce-scatter.16
where the time goes:
time: 1270 us
  waiting for transfers between devices  798 us (63%)
  matrix products  174 us (14%)
  blocking collectives  146 us (11%)
  local copies, waits for them, and re-layouts  76.5 us (6%)
  other arithmetic  55 us (4%)
  between operations  15.2 us (1%)
    reduce_scatter x6, waiting for transfers between devices, scatter_matrix(): lax.psum_scatter(halves, ('tensor', 'dp'), scatter_dimension=0, tiled=True)  664 us
    all_gather x6, waiting for transfers between devices, gather_matrix(): return lax.all_gather(wide, 'dp', axis=0, tiled=True)  134 us
    dot_general x18, matrix products, mm(): return lax.dot_general(a, b, (dims, ((), ())), preferred_element_type=f32)  125 us
    all_gather x1, blocking collectives, shards(): packed = lax.all_gather(jnp.concatenate(vectors), BOTH, axis=0)  65.8 us
    all_gather x6, blocking collectives, gather_matrix(): wide = lax.all_gather(shard, 'tensor', axis=1, tiled=True)  40.1 us
    unnamed x1, blocking collectives  39.9 us
    reshape x8, local copies, waits for them, and re-layouts, split(): return rows.reshape(image_count, slot_count, heads, HEAD_DIM)  36.3 us
  transfers between devices with their start and end apart: 12, of which 8 were waited for; matrix products, arithmetic and copies ran while one was open for 18% of the time, Pallas kernels for 0%

commit v1 on v0

--- a/solution.py
+++ b/solution.py
@@ -8,6 +8,28 @@
 BOTH = ("dp", "tensor")
 bf16 = jnp.bfloat16
 f32 = jnp.float32
+
+
+def pages_fit(body, dim_i):
+    body = jnp.moveaxis(body, 0, dim_i)
+    v1 = body.shape
+    return body.reshape(*v1[:dim_i], v1[dim_i] * v1[dim_i + 1], *v1[dim_i + 2 :])
+
+
+def zone_measure(my_data, named_axis):
+    all_values = my_data[None]
+    n_chips = lax.axis_size(named_axis)
+    for kk in range(n_chips.bit_length() - 1):
+        out_arr = 1 << kk
+        t_next = lax.ppermute(
+            all_values,
+            axis_name=named_axis,
+            perm=tuple(((pp, pp ^ out_arr) for pp in range(n_chips))),
+        )
+        upper = jnp.stack([all_values, t_next], axis=0)
+        heard = lax.axis_index(named_axis) >> kk & 1
+        all_values = jnp.where(heard == 0, upper, upper[::-1]).reshape(-1, *my_data.shape)
+    return all_values
 
 
 def exact_gelu(values):
@@ -31,7 +53,11 @@
 
 def gather_matrix(shard):
     wide = lax.all_gather(shard, "tensor", axis=1, tiled=True)
-    return lax.all_gather(wide, "dp", axis=0, tiled=True)
+
+    def draw_the_hubs(obj, point, axis_no):
+        return pages_fit(zone_measure(obj, point), axis_no)
+
+    return draw_the_hubs(wide, "dp", 0)
 
 
 def scatter_matrix(grad):

time: 1270 us -> 1780 us (1.40)
  waiting for transfers between devices: 798 us -> 1220 us
  other arithmetic: 55 us -> 118 us
    ppermute x0 -> x24, waiting for transfers between devices: none -> 543 us  [zone_measure(): lax.ppermute(all_values, axis_name=named_axis, perm=tuple(((pp, pp ^ out_...]
    all_gather x6 -> x0, waiting for transfers between devices: 134 us -> none  [gather_matrix(): return lax.all_gather(wide, 'dp', axis=0, tiled=True)]
    select_n x0 -> x18, other arithmetic: none -> 43.6 us  [zone_measure(): jnp.where(heard == 0, upper, upper[::-1]).reshape(-1, *my_data.shape)]
    another operation x0 -> x30, other arithmetic: none -> 28 us  [zone_measure(): upper = jnp.stack([all_values, t_next], axis=0)]
  transfers between devices with their start and end apart: 12 -> 30, of which waited for: 8 -> 14; matrix products, arithmetic and copies ran while one was open for 18% -> 14% of each run, Pallas kernels for 0% -> 0%
where the time goes in v1:
time: 1780 us; the launch traced here: 1770 us
  waiting for transfers between devices  1220 us (69%)
  matrix products  170 us (10%)
  blocking collectives  146 us (8%)
  other arithmetic  118 us (7%)
  local copies, waits for them, and re-layouts  84.4 us (5%)
  starting transfers between devices  18 us (1%)
    reduce_scatter x6, waiting for transfers between devices, scatter_matrix(): lax.psum_scatter(halves, ('tensor', 'dp'), scatter_dimension=0, tiled=True)  680 us
    ppermute x24, waiting for transfers between devices, zone_measure(): lax.ppermute(all_values, axis_name=named_axis, perm=tuple(((pp, pp ^ out_...  543 us
    dot_general x18, matrix products, mm(): return lax.dot_general(a, b, (dims, ((), ())), preferred_element_type=f32)  128 us
    all_gather x1, blocking collectives, shards(): packed = lax.all_gather(jnp.concatenate(vectors), BOTH, axis=0)  69.3 us
    select_n x18, other arithmetic, zone_measure(): jnp.where(heard == 0, upper, upper[::-1]).reshape(-1, *my_data.shape)  43.6 us
    all_gather x6, blocking collectives, gather_matrix(): wide = lax.all_gather(shard, 'tensor', axis=1, tiled=True)  38.7 us
    unnamed x1, blocking collectives  37.6 us
    reshape x8, local copies, waits for them, and re-layouts, split(): return rows.reshape(image_count, slot_count, heads, HEAD_DIM)  36.8 us
  transfers between devices with their start and end apart: 30, of which 14 were waited for; matrix products, arithmetic and copies ran while one was open for 14% of the time, Pallas kernels for 0%

profile of v1, /device:TPU:0, one launch (start us, length us, event | category | flops | bytes accessed | tf_op | source)
XLA Modules:
  0.0 1774.7 jit_solution(11829527573890441382)
XLA Ops:
  7.2 6.3 all_gather.29
  30.2 9.6 all_gather.31
  45.9 69.3 %all-gather.4 = bf16[32,1,384]{2,1,0:T(2,128)(2,1)S(1)} all-gather(bf16[1,1,384]{2,1,0:T(2,128)(2,1)S(1)} %reshape.578), channel_id=2, replica_groups=mesh['dp'=16,'tensor'=2] {'dp','tensor'}, dimensions={0}, use_global_device_ids=true | all-gather | bytes 25344 | tf_op jit(solution)/shard_map/all_gather | solution.py:115
  130.0 7.0 all_gather.30
  140.6 17.5 collective-permute-done.9
  158.5 7.4 collective-permute-done.1
  172.1 31.2 %collective-permute-done.6 = bf16[4,64,1024]{2,1,0:T(8,128)(2,1)S(1)} collective-permute-done((bf16[4,64,1024]{2,1,0:T(8,128)(2,1)S(1)}, bf16[4,64,1024]{2,1,0:T(8,128)(2,1)S(1)}, u32[]{:S(2)}, u32[]{:S(2)}) %collective-permute-start.6) | collective-permute-done | bytes 524320 | tf_op jit(solution)/shard_map/ppermute | solution.py:24
  203.9 8.4 collective-permute-done.14
  225.5 125.0 %collective-permute-done.7 = bf16[8,64,1024]{2,1,0:T(8,128)(2,1)S(1)} collective-permute-done((bf16[8,64,1024]{2,1,0:T(8,128)(2,1)S(1)}, bf16[8,64,1024]{2,1,0:T(8,128)(2,1)S(1)}, u32[]{:S(2)}, u32[]{:S(2)}) %collective-permute-start.7) | collective-permute-done | bytes 1048608 | tf_op jit(solution)/shard_map/ppermute | solution.py:24
  364.8 30.8 %collective-permute-done.11 = bf16[8,64,1024]{2,1,0:T(8,128)(2,1)} collective-permute-done((bf16[8,64,1024]{2,1,0:T(8,128)(2,1)}, bf16[8,64,1024]{2,1,0:T(8,128)(2,1)}, u32[]{:S(2)}, u32[]{:S(2)}) %collective-permute-start.11) | collective-permute-done | bytes 1048608 | tf_op jit(solution)/shard_map/ppermute | solution.py:24
  414.7 11.1 fusion.61
  465.0 253.7 %collective-permute-done.23 = bf16[8,64,4096]{2,1,0:T(8,128)(2,1)} collective-permute-done((bf16[8,64,4096]{2,1,0:T(8,128)(2,1)}, bf16[8,64,4096]{2,1,0:T(8,128)(2,1)}, u32[]{:S(2)}, u32[]{:S(2)}) %collective-permute-start.23) | collective-permute-done | bytes 4194336 | tf_op jit(solution)/shard_map/ppermute | solution.py:24
  718.6 7.4 pad_maximum_fusion.1
  726.1 13.5 reverse_select_fusion
  739.5 68.9 %collective-permute-done.19 = bf16[8,64,4096]{2,1,0:T(8,128)(2,1)} collective-permute-done((bf16[8,64,4096]{2,1,0:T(8,128)(2,1)}, bf16[8,64,4096]{2,1,0:T(8,128)(2,1)}, u32[]{:S(2)}, u32[]{:S(2)}) %collective-permute-start.19) | collective-permute-done | bytes 4194336 | tf_op jit(solution)/shard_map/ppermute | solution.py:24
  808.4 7.4 pad_maximum_fusion
  815.9 13.7 reverse_select_fusion.1
  829.6 33.5 %multiply_convert_fusion.1 = (bf16[640,4096]{1,0:T(8,128)(2,1)}, f32[640,4096]{1,0:T(8,128)}, f32[640,4096]{1,0:T(8,128)}) fusion(f32[4096]{0:T(1024)S(1)} %copy-done.35, bf16[1024,4096]{1,0:T(8,128)(2,1)} %bitcast.278, f32[640,1024]{1,0:T(8,128)S(1)} %get-tuple-element.75, f32[1024]{0:T(1024)S(1)} %copy-done.36, f32[1024]{0:T(1024)S(1)} %copy-done.31, ...), kind=kOutput, calls=%fused_computation.20 | convolution fusion | flops 5545000960 | bytes 37254144 | tf_op jit(solution)/shard_map/dot_general | solution.py:71
  863.1 16.3 convert_reduce_fusion
  879.4 10.7 multiply_reduce_fusion.1
  903.8 8.6 convert_reduce_fusion.1
  922.0 13.8 multiply_reduce_fusion
  935.9 11.0 multiply_convert_fusion
  978.8 10.0 convolution_convert_fusion
  997.9 9.5 convert_bitcast_fusion
  1027.2 37.6 %all-reduce = f32[32,384]{1,0:T(8,128)S(1)} all-reduce(f32[32,384]{1,0:T(8,128)S(1)} %concatenate.7), channel_id=6, replica_groups=mesh['dp'=16,'tensor'=2] {'dp','tensor'}, use_global_device_ids=true, to_apply=%region_20.21.clone | all-reduce | flops 12288 | bytes 98304
  1070.4 10.5 add_convert_fusion
  1080.8 114.0 %reduce-scatter.9.cloned.1.call-done = bf16[64,512]{1,0:T(8,128)(2,1)} async-done(((bf16[2048,512]{1,0:T(8,128)(2,1)}), bf16[64,512]{1,0:T(8,128)(2,1)}) %reduce-scatter.9.cloned.1.call-update) | async-done | bytes 65552 | tf_op jit(solution)/shard_map/reduce_scatter | solution.py:67
  1194.8 137.1 %reduce-scatter.7.cloned.1.call-done = bf16[64,512]{1,0:T(8,128)(2,1)} async-done(((bf16[2048,512]{1,0:T(8,128)(2,1)}), bf16[64,512]{1,0:T(8,128)(2,1)}) %reduce-scatter.7.cloned.1.call-update) | async-done | bytes 65552 | tf_op jit(solution)/shard_map/reduce_scatter | solution.py:67
  1333.6 135.4 %reduce-scatter.13.cloned.1.call-done = bf16[64,512]{1,0:T(8,128)(2,1)} async-done(((bf16[2048,512]{1,0:T(8,128)(2,1)}), bf16[64,512]{1,0:T(8,128)(2,1)}) %reduce-scatter.13.cloned.1.call-update) | async-done | bytes 65552 | tf_op jit(solution)/shard_map/reduce_scatter | solution.py:67
  1470.5 146.9 %reduce-scatter.15.cloned.1.call-done = bf16[64,2048]{1,0:T(8,128)(2,1)} async-done(((bf16[2048,2048]{1,0:T(8,128)(2,1)}), bf16[64,2048]{1,0:T(8,128)(2,1)}) %reduce-scatter.15.cloned.1.call-update) | async-done | bytes 262160 | tf_op jit(solution)/shard_map/reduce_scatter | solution.py:67
  1619.2 146.7 %reduce-scatter.17.cloned.1.call-done = bf16[64,2048]{1,0:T(8,128)(2,1)} async-done(((bf16[2048,2048]{1,0:T(8,128)(2,1)}), bf16[64,2048]{1,0:T(8,128)(2,1)}) %reduce-scatter.17.cloned.1.call-update) | async-done | bytes 262160 | tf_op jit(solution)/shard_map/reduce_scatter | solution.py:67
  (284 shorter events, 229.7 us)
Async XLA Ops:
  7.2 1073.7 %reduce-scatter.11.cloned.1.call-start = ((), (), s32[]{:S(2)}) async-start(), calls=%async_computation.8 | async-start | bytes 2162688 | tf_op jit(solution)/shard_map/reduce_scatter | solution.py:67
  13.5 123.5 %collective-permute-start.12 = (bf16[1,64,1024]{2,1,0:T(8,128)(2,1)S(1)}, bf16[1,64,1024]{2,1,0:T(8,128)(2,1)}, u32[]{:S(2)}, u32[]{:S(2)}) collective-permute-start(bf16[1,64,1024]{2,1,0:T(8,128)(2,1)S(1)} %bitcast.323), channel_id=1, source_target_pairs={{0,2},{2,0},{4,6},{6,4},{8,10},{10,8},{12,14},{14,12},{16,18},{18,... | collective-permute-start | bytes 393224 | tf_op jit(solution)/shard_map/ppermute | solution.py:24
  19.9 118.2 %collective-permute-start.4 = (bf16[1,64,1024]{2,1,0:T(8,128)(2,1)S(1)}, bf16[1,64,1024]{2,1,0:T(8,128)(2,1)S(1)}, u32[]{:S(2)}, u32[]{:S(2)}) collective-permute-start(bf16[1,64,1024]{2,1,0:T(8,128)(2,1)S(1)} %all-gather.2), channel_id=1, source_target_pairs={{0,2},{2,0},{4,6},{6,4},{8,10},{10,8},{12,14},{14,12},{16,18},{18,... | collective-permute-start | bytes 393224 | tf_op jit(solution)/shard_map/ppermute | solution.py:24
  25.0 115.4 %collective-permute-start = (bf16[1,64,1024]{2,1,0:T(8,128)(2,1)S(1)}, bf16[1,64,1024]{2,1,0:T(8,128)(2,1)S(1)}, u32[]{:S(2)}, u32[]{:S(2)}) collective-permute-start(bf16[1,64,1024]{2,1,0:T(8,128)(2,1)S(1)} %all-gather.1), channel_id=1, source_target_pairs={{0,2},{2,0},{4,6},{6,4},{8,10},{10,8},{12,14},{14,12},{16,18},{18,... | collective-permute-start | bytes 393224 | tf_op jit(solution)/shard_map/ppermute | solution.py:24
  30.2 108.1 %collective-permute-start.8 = (bf16[1,64,1024]{2,1,0:T(8,128)(2,1)S(1)}, bf16[1,64,1024]{2,1,0:T(8,128)(2,1)S(1)}, u32[]{:S(2)}, u32[]{:S(2)}) collective-permute-start(bf16[1,64,1024]{2,1,0:T(8,128)(2,1)S(1)} %all-gather.3), channel_id=1, source_target_pairs={{0,2},{2,0},{4,6},{6,4},{8,10},{10,8},{12,14},{14,12},{16,18},{18,... | collective-permute-start | bytes 393224 | tf_op jit(solution)/shard_map/ppermute | solution.py:24
  39.8 131.3 %collective-permute-start.20 = (bf16[1,64,4096]{2,1,0:T(8,128)(2,1)S(1)}, bf16[1,64,4096]{2,1,0:T(8,128)(2,1)S(1)}, u32[]{:S(2)}, u32[]{:S(2)}) collective-permute-start(bf16[1,64,4096]{2,1,0:T(8,128)(2,1)S(1)} %bitcast.299), channel_id=1, source_target_pairs={{0,2},{2,0},{4,6},{6,4},{8,10},{10,8},{12,14},{14,12},{16,18},{18,... | collective-permute-start | bytes 1572872 | tf_op jit(solution)/shard_map/ppermute | solution.py:24
  130.0 221.3 %copy-start.17 = (bf16[2,320,1024]{2,1,0:T(8,128)(2,1)}, bf16[2,320,1024]{2,1,0:T(8,128)(2,1)S(1)}, u32[]{:S(2)}) copy-start(bf16[2,320,1024]{2,1,0:T(8,128)(2,1)S(1)} %add_convert_fusion.4) | copy-start | bytes 3932164
  137.1 31.6 %collective-permute-start.16 = (bf16[1,64,4096]{2,1,0:T(8,128)(2,1)S(1)}, bf16[1,64,4096]{2,1,0:T(8,128)(2,1)S(1)}, u32[]{:S(2)}, u32[]{:S(2)}) collective-permute-start(bf16[1,64,4096]{2,1,0:T(8,128)(2,1)S(1)} %bitcast.301), channel_id=1, source_target_pairs={{0,2},{2,0},{4,6},{6,4},{8,10},{10,8},{12,14},{14,12},{16,18},{18,... | collective-permute-start | bytes 1572872 | tf_op jit(solution)/shard_map/ppermute | solution.py:24
  138.1 30.3 %collective-permute-start.13 = (bf16[2,64,1024]{2,1,0:T(8,128)(2,1)S(1)}, bf16[2,64,1024]{2,1,0:T(8,128)(2,1)S(1)}, u32[]{:S(2)}, u32[]{:S(2)}) collective-permute-start(bf16[2,64,1024]{2,1,0:T(8,128)(2,1)S(1)} %get-tuple-element.44), channel_id=1, source_target_pairs={{0,4},{2,6},{4,0},{6,2},{8,12},{10,14},{12,8},{14,10},{16,20},{18,... | collective-permute-start | bytes 786440 | tf_op jit(solution)/shard_map/ppermute | solution.py:24
  138.3 27.9 %collective-permute-start.5 = (bf16[2,64,1024]{2,1,0:T(8,128)(2,1)S(1)}, bf16[2,64,1024]{2,1,0:T(8,128)(2,1)S(1)}, u32[]{:S(2)}, u32[]{:S(2)}) collective-permute-start(bf16[2,64,1024]{2,1,0:T(8,128)(2,1)S(1)} %get-tuple-element.48), channel_id=1, source_target_pairs={{0,4},{2,6},{4,0},{6,2},{8,12},{10,14},{12,8},{14,10},{16,20},{18,... | collective-permute-start | bytes 786440 | tf_op jit(solution)/shard_map/ppermute | solution.py:24
  140.5 17.6 collective-permute-start.9
  158.1 7.9 collective-permute-start.1
  165.9 52.2 %collective-permute-start.10 = (bf16[4,64,1024]{2,1,0:T(8,128)(2,1)S(1)}, bf16[4,64,1024]{2,1,0:T(8,128)(2,1)S(1)}, u32[]{:S(2)}, u32[]{:S(2)}) collective-permute-start(bf16[4,64,1024]{2,1,0:T(8,128)(2,1)S(1)} %bitcast.303), channel_id=1, source_target_pairs={{0,8},{2,10},{4,12},{6,14},{8,0},{10,2},{12,4},{14,6},{16,24},{18,... | collective-permute-start | bytes 1572872 | tf_op jit(solution)/shard_map/ppermute | solution.py:24
  166.1 47.8 %collective-permute-start.2 = (bf16[4,64,1024]{2,1,0:T(8,128)(2,1)S(1)}, bf16[4,64,1024]{2,1,0:T(8,128)(2,1)S(1)}, u32[]{:S(2)}, u32[]{:S(2)}) collective-permute-start(bf16[4,64,1024]{2,1,0:T(8,128)(2,1)S(1)} %bitcast.305), channel_id=1, source_target_pairs={{0,8},{2,10},{4,12},{6,14},{8,0},{10,2},{12,4},{14,6},{16,24},{18,... | collective-permute-start | bytes 1572872 | tf_op jit(solution)/shard_map/ppermute | solution.py:24
  168.4 34.8 %collective-permute-start.6 = (bf16[4,64,1024]{2,1,0:T(8,128)(2,1)S(1)}, bf16[4,64,1024]{2,1,0:T(8,128)(2,1)S(1)}, u32[]{:S(2)}, u32[]{:S(2)}) collective-permute-start(bf16[4,64,1024]{2,1,0:T(8,128)(2,1)S(1)} %bitcast.307), channel_id=1, source_target_pairs={{0,8},{2,10},{4,12},{6,14},{8,0},{10,2},{12,4},{14,6},{16,24},{18,... | collective-permute-start | bytes 1572872 | tf_op jit(solution)/shard_map/ppermute | solution.py:24
  168.7 43.6 %collective-permute-start.14 = (bf16[4,64,1024]{2,1,0:T(8,128)(2,1)S(1)}, bf16[4,64,1024]{2,1,0:T(8,128)(2,1)S(1)}, u32[]{:S(2)}, u32[]{:S(2)}) collective-permute-start(bf16[4,64,1024]{2,1,0:T(8,128)(2,1)S(1)} %bitcast.309), channel_id=1, source_target_pairs={{0,8},{2,10},{4,12},{6,14},{8,0},{10,2},{12,4},{14,6},{16,24},{18,... | collective-permute-start | bytes 1572872 | tf_op jit(solution)/shard_map/ppermute | solution.py:24
  171.4 48.1 %collective-permute-start.21 = (bf16[2,64,4096]{2,1,0:T(8,128)(2,1)S(1)}, bf16[2,64,4096]{2,1,0:T(8,128)(2,1)S(1)}, u32[]{:S(2)}, u32[]{:S(2)}) collective-permute-start(bf16[2,64,4096]{2,1,0:T(8,128)(2,1)S(1)} %get-tuple-element.40), channel_id=1, source_target_pairs={{0,4},{2,6},{4,0},{6,2},{8,12},{10,14},{12,8},{14,10},{16,20},{18,... | collective-permute-start | bytes 3145736 | tf_op jit(solution)/shard_map/ppermute | solution.py:24
  203.2 21.2 %collective-permute-start.17 = (bf16[2,64,4096]{2,1,0:T(8,128)(2,1)S(1)}, bf16[2,64,4096]{2,1,0:T(8,128)(2,1)S(1)}, u32[]{:S(2)}, u32[]{:S(2)}) collective-permute-start(bf16[2,64,4096]{2,1,0:T(8,128)(2,1)S(1)} %get-tuple-element.42), channel_id=1, source_target_pairs={{0,4},{2,6},{4,0},{6,2},{8,12},{10,14},{12,8},{14,10},{16,20},{18,... | collective-permute-start | bytes 3145736 | tf_op jit(solution)/shard_map/ppermute | solution.py:24
  213.9 245.6 %collective-permute-start.15 = (bf16[8,64,1024]{2,1,0:T(8,128)(2,1)}, bf16[8,64,1024]{2,1,0:T(8,128)(2,1)}, u32[]{:S(2)}, u32[]{:S(2)}) collective-permute-start(bf16[8,64,1024]{2,1,0:T(8,128)(2,1)} %bitcast.54), channel_id=1, source_target_pairs={{0,16},{2,18},{4,20},{6,22},{8,24},{10,26},{12,28},{14,30},{16,0},... | collective-permute-start | bytes 3145736 | tf_op jit(solution)/shard_map/ppermute | solution.py:24
  213.9 136.6 %collective-permute-start.7 = (bf16[8,64,1024]{2,1,0:T(8,128)(2,1)S(1)}, bf16[8,64,1024]{2,1,0:T(8,128)(2,1)S(1)}, u32[]{:S(2)}, u32[]{:S(2)}) collective-permute-start(bf16[8,64,1024]{2,1,0:T(8,128)(2,1)S(1)} %bitcast.288), channel_id=1, source_target_pairs={{0,16},{2,18},{4,20},{6,22},{8,24},{10,26},{12,28},{14,30},{16,0},... | collective-permute-start | bytes 3145736 | tf_op jit(solution)/shard_map/ppermute | solution.py:24
  218.2 192.9 %collective-permute-start.3 = (bf16[8,64,1024]{2,1,0:T(8,128)(2,1)}, bf16[8,64,1024]{2,1,0:T(8,128)(2,1)}, u32[]{:S(2)}, u32[]{:S(2)}) collective-permute-start(bf16[8,64,1024]{2,1,0:T(8,128)(2,1)} %bitcast.12), channel_id=1, source_target_pairs={{0,16},{2,18},{4,20},{6,22},{8,24},{10,26},{12,28},{14,30},{16,0},... | collective-permute-start | bytes 3145736 | tf_op jit(solution)/shard_map/ppermute | solution.py:24
  219.6 176.0 %collective-permute-start.11 = (bf16[8,64,1024]{2,1,0:T(8,128)(2,1)}, bf16[8,64,1024]{2,1,0:T(8,128)(2,1)}, u32[]{:S(2)}, u32[]{:S(2)}) collective-permute-start(bf16[8,64,1024]{2,1,0:T(8,128)(2,1)} %bitcast.38), channel_id=1, source_target_pairs={{0,16},{2,18},{4,20},{6,22},{8,24},{10,26},{12,28},{14,30},{16,0},... | collective-permute-start | bytes 3145736 | tf_op jit(solution)/shard_map/ppermute | solution.py:24
  225.1 221.0 %collective-permute-start.18 = (bf16[4,64,4096]{2,1,0:T(8,128)(2,1)S(1)}, bf16[4,64,4096]{2,1,0:T(8,128)(2,1)}, u32[]{:S(2)}, u32[]{:S(2)}) collective-permute-start(bf16[4,64,4096]{2,1,0:T(8,128)(2,1)S(1)} %bitcast.284), channel_id=1, source_target_pairs={{0,8},{2,10},{4,12},{6,14},{8,0},{10,2},{12,4},{14,6},{16,24},{18,... | collective-permute-start | bytes 6291464 | tf_op jit(solution)/shard_map/ppermute | solution.py:24
  350.5 89.9 %collective-permute-start.22 = (bf16[4,64,4096]{2,1,0:T(8,128)(2,1)}, bf16[4,64,4096]{2,1,0:T(8,128)(2,1)}, u32[]{:S(2)}, u32[]{:S(2)}) collective-permute-start(bf16[4,64,4096]{2,1,0:T(8,128)(2,1)} %bitcast.81), channel_id=1, source_target_pairs={{0,8},{2,10},{4,12},{6,14},{8,0},{10,2},{12,4},{14,6},{16,24},{18,... | collective-permute-start | bytes 6291464 | tf_op jit(solution)/shard_map/ppermute | solution.py:24
  446.1 272.5 %collective-permute-start.23 = (bf16[8,64,4096]{2,1,0:T(8,128)(2,1)}, bf16[8,64,4096]{2,1,0:T(8,128)(2,1)}, u32[]{:S(2)}, u32[]{:S(2)}) collective-permute-start(bf16[8,64,4096]{2,1,0:T(8,128)(2,1)} %bitcast.84), channel_id=1, source_target_pairs={{0,16},{2,18},{4,20},{6,22},{8,24},{10,26},{12,28},{14,30},{16,0},... | collective-permute-start | bytes 12582920 | tf_op jit(solution)/shard_map/ppermute | solution.py:24
  451.2 357.2 %collective-permute-start.19 = (bf16[8,64,4096]{2,1,0:T(8,128)(2,1)}, bf16[8,64,4096]{2,1,0:T(8,128)(2,1)}, u32[]{:S(2)}, u32[]{:S(2)}) collective-permute-start(bf16[8,64,4096]{2,1,0:T(8,128)(2,1)} %bitcast.68), channel_id=1, source_target_pairs={{0,16},{2,18},{4,20},{6,22},{8,24},{10,26},{12,28},{14,30},{16,0},... | collective-permute-start | bytes 12582920 | tf_op jit(solution)/shard_map/ppermute | solution.py:24
  464.5 425.6 %copy-start.3 = (f32[640,1024]{1,0:T(8,128)}, f32[640,1024]{1,0:T(8,128)S(1)}, u32[]{:S(2)}) copy-start(f32[640,1024]{1,0:T(8,128)S(1)} %get-tuple-element.75) | copy-start | bytes 7864324
  921.5 273.4 %reduce-scatter.9.cloned.1.call-start = ((), (), s32[]{:S(2)}) async-start(), calls=%async_computation.7 | async-start | bytes 2162688 | tf_op jit(solution)/shard_map/reduce_scatter | solution.py:67
  958.8 373.1 %reduce-scatter.7.cloned.1.call-start = ((), (), s32[]{:S(2)}) async-start(), calls=%async_computation.6 | async-start | bytes 2162688 | tf_op jit(solution)/shard_map/reduce_scatter | solution.py:67
  973.2 495.8 %reduce-scatter.13.cloned.1.call-start = ((), (), s32[]{:S(2)}) async-start(), calls=%async_computation.9 | async-start | bytes 2162688 | tf_op jit(solution)/shard_map/reduce_scatter | solution.py:67
  978.7 638.7 %reduce-scatter.15.cloned.1.call-start = ((), (), s32[]{:S(2)}) async-start(), calls=%async_computation.10 | async-start | bytes 8650752 | tf_op jit(solution)/shard_map/reduce_scatter | solution.py:67
  997.4 768.5 %reduce-scatter.17.cloned.1.call-start = ((), (), s32[]{:S(2)}) async-start(), calls=%async_computation.11 | async-start | bytes 8650752 | tf_op jit(solution)/shard_map/reduce_scatter | solution.py:67
  (44 other events, 389.8 us)
Sparse Core Ops, SparseCore 0:
  921.6 136.1 reduce-scatter.10
  1060.1 134.6 reduce-scatter.8
  1197.1 134.7 reduce-scatter.6
  1334.0 134.9 reduce-scatter.12
  1471.1 146.2 reduce-scatter.14
  1619.6 146.3 reduce-scatter.16
